TPU v7x, 32 devices: a whole 2x2x4 slice. The times are simulated.
32 devices in a mesh: face: 4 (over x, core), sub: 8 (over z, y).
Axes of the slice: x: 2, y: 2, z: 4, core: 2. Of those that a mesh axis runs over, the one named last changes fastest.
Arguments:
- grid_latent: bfloat16 [16384, 512], P(('face', 'sub')), may hold values from -6 to 6
- mesh_latent: bfloat16 [4096, 512], P(('face', 'sub')), may hold values from -6 to 6
- edge_latent: bfloat16 [32768, 512], P(('face', 'sub')), may hold values from -6 to 6
- mesh_cotangent: bfloat16 [4096, 512], P(('face', 'sub')), may hold values from -6 to 6
- edge_cotangent: bfloat16 [32768, 512], P(('face', 'sub')), may hold values from -6 to 6
- grid_send: int32 [32, 4, 256], P(('face', 'sub')), may hold values from 0 to 511
- grid_slot: int32 [32768], P(('face', 'sub')), may hold values from 0 to 1535, as said below
- grid_target: int32 [32768], P(('face', 'sub')), may hold values from 0 to 127
- mesh_halo: int32 [32, 4, 64], P(('face', 'sub')), may hold values from 0 to 127
- mesh_send: int32 [32, 32, 4], P(('face', 'sub')), may hold values from 0 to 127
- mesh_slot: int32 [32768], P(('face', 'sub')), may hold values from 0 to 511, as said below
- mesh_target: int32 [32768], P(('face', 'sub')), may hold values from 0 to 127
- weights: bfloat16 [10, 512, 512], replicated, may hold values from -0.25 to 0.25
Outputs:
- mesh_update: bfloat16 [4096, 512], P(('face', 'sub'))
- grid_grad: bfloat16 [16384, 512], P(('face', 'sub'))
- mesh_grad: bfloat16 [4096, 512], P(('face', 'sub'))
- edge_grad: bfloat16 [32768, 512], P(('face', 'sub'))
- weight_grads: bfloat16 [10, 512, 512], replicated
Inputs may be any that keep to these rules, and one draw needn't show every extreme that they name: grid_slot[e] names the edge device's own 512 grid rows or, above them, the 256 rows listed by each of its four neighbours in direction order. grid_target[e] is local to the edge's device. grid_send[q, k] lists local rows of device q for the device d with nb(d, k) = q; a row may appear in several slots. mesh_slot[e] names the own 128 mesh rows, then the 64 rows listed by each of the four neighbours, then 4 far rows from each device, source major. mesh_target[e] is local to the edge's device. mesh_halo[q, k] lists local rows of device q for its neighbour in direction k. mesh_send[q, d] lists local rows of device q for far edges of device d.
All inputs are finite; a program needn't handle non-finite values.
Results may differ from a plain program's by a relative error of at most 0.016.
Values may be sent and summed in bfloat16 or wider, within the bound.
A program may use at most 128 MiB of HBM per device.

v0:
```python
import jax
import jax.numpy as jnp
from jax import lax
from jax.sharding import PartitionSpec as P

norm_eps = 1e-05


def shifted(value, axis, steps):
    count = lax.axis_size(axis)
    pairs = [(source, (source + steps) % count) for source in range(count)]
    return lax.ppermute(value, axis, pairs)


def layer_norm(values):
    centre = values - jnp.mean(values, axis=-1, keepdims=True)
    spread = jnp.mean(centre * centre, axis=-1, keepdims=True)
    return centre * lax.rsqrt(spread + norm_eps)


def layer_norm_back(values, upstream):
    centre = values - jnp.mean(values, axis=-1, keepdims=True)
    inverse = lax.rsqrt(jnp.mean(centre * centre, axis=-1, keepdims=True) + norm_eps)
    normed = centre * inverse
    return inverse * (
        upstream
        - jnp.mean(upstream, axis=-1, keepdims=True)
        - normed * jnp.mean(upstream * normed, axis=-1, keepdims=True)
    )


def swish_slope(values):
    sigmoid_values = jax.nn.sigmoid(values)
    return sigmoid_values * (1.0 + values * (1.0 - sigmoid_values))


def product(former, latter):
    return jnp.dot(former, latter, preferred_element_type=jnp.float32)


def outer_sum(former, latter):
    return lax.dot_general(
        former, latter, (((0,), (0,)), ((), ())), preferred_element_type=jnp.float32
    )


def back_product(former, latter):
    return lax.dot_general(
        former, latter, (((1,), (1,)), ((), ())), preferred_element_type=jnp.float32
    )


def receive_sum(onehot, values):
    upper = values.astype(jnp.bfloat16)
    lower = (values - upper.astype(jnp.float32)).astype(jnp.bfloat16)
    return outer_sum(onehot, upper) + outer_sum(onehot, lower)


def grid_neighbours(outgoing):
    from_sub = [shifted(outgoing[block], "sub", offset) for block, offset in ((0, 1), (1, -1))]
    from_face = [shifted(outgoing[block], "face", offset) for block, offset in ((2, 1), (3, -1))]
    return jnp.concatenate(from_sub + from_face, axis=0)


def grid_returns(partials):
    to_sub = [shifted(partials[block], "sub", offset) for block, offset in ((0, -1), (1, 1))]
    to_face = [shifted(partials[block], "face", offset) for block, offset in ((2, -1), (3, 1))]
    return jnp.concatenate(to_sub + to_face, axis=0)


def mesh_neighbours(outgoing):
    from_sub = [shifted(outgoing[block], "sub", offset) for block, offset in ((0, 1), (1, -1))]
    from_face = [shifted(outgoing[block], "face", offset) for block, offset in ((2, 1), (3, -1))]
    return jnp.concatenate(from_sub + from_face, axis=0)


def mesh_returns(partials):
    to_sub = [shifted(partials[block], "sub", offset) for block, offset in ((0, -1), (1, 1))]
    to_face = [shifted(partials[block], "face", offset) for block, offset in ((2, -1), (3, 1))]
    return jnp.concatenate(to_sub + to_face, axis=0)


def move_mesh(outgoing):
    return lax.all_to_all(outgoing, ("face", "sub"), split_axis=0, concat_axis=0, tiled=True)


def return_mesh(outgoing):
    return lax.all_to_all(outgoing, ("face", "sub"), split_axis=0, concat_axis=0, tiled=True)


def on_device(
    grid_latent,
    mesh_latent,
    edge_latent,
    mesh_cotangent,
    edge_cotangent,
    grid_send,
    grid_slot,
    grid_target,
    mesh_halo,
    mesh_send,
    mesh_slot,
    mesh_target,
    weights,
):
    peer_count = lax.axis_size("face") * lax.axis_size("sub")
    latent = weights.shape[1]
    mesh_rows = mesh_latent.shape[0]
    grid_rows = grid_latent.shape[0]
    grid_table = grid_send[0].reshape(-1)
    halo_table = mesh_halo[0].reshape(-1)
    far_table = mesh_send[0].reshape(-1)
    halo_count = halo_table.shape[0]
    node_ids = jnp.arange(mesh_rows, dtype=jnp.int32)
    grid_project = product(grid_latent, weights[0]).astype(jnp.bfloat16)
    grid_outgoing = jnp.take(grid_project, grid_table, axis=0).reshape(4, -1, latent)
    grid_source = jnp.concatenate([grid_project, grid_neighbours(grid_outgoing)], axis=0)
    encode_receive = product(mesh_latent, weights[1])
    encoder_pre = jnp.take(grid_source, grid_slot, axis=0).astype(jnp.float32) + jnp.take(
        encode_receive, grid_target, axis=0
    )
    encoder_hidden = jax.nn.silu(encoder_pre).astype(jnp.bfloat16)
    encoder_linear = product(encoder_hidden, weights[2])
    encoder_message = layer_norm(encoder_linear).astype(jnp.bfloat16)
    grid_onehot = (grid_target[:, None] == node_ids[None, :]).astype(jnp.bfloat16)
    encoder_total = outer_sum(grid_onehot, encoder_message)
    mesh_middle = (mesh_latent.astype(jnp.float32) + encoder_total).astype(jnp.bfloat16)
    sender_rows = product(mesh_middle, weights[4]).astype(jnp.bfloat16)
    halo_outgoing = jnp.take(sender_rows, halo_table, axis=0).reshape(4, -1, latent)
    far_outgoing = jnp.take(sender_rows, far_table, axis=0).reshape(peer_count, -1, latent)
    far_incoming = move_mesh(far_outgoing).reshape(-1, latent)
    mesh_source = jnp.concatenate(
        [sender_rows, mesh_neighbours(halo_outgoing), far_incoming], axis=0
    )
    process_receive = product(mesh_middle, weights[5])
    process_pre = (
        product(edge_latent, weights[3])
        + jnp.take(mesh_source, mesh_slot, axis=0).astype(jnp.float32)
        + jnp.take(process_receive, mesh_target, axis=0)
    )
    process_hidden = jax.nn.silu(process_pre).astype(jnp.bfloat16)
    process_linear = product(process_hidden, weights[6])
    edge_update = layer_norm(process_linear).astype(jnp.bfloat16)
    mesh_onehot = (mesh_target[:, None] == node_ids[None, :]).astype(jnp.bfloat16)
    process_round = outer_sum(mesh_onehot, edge_update).astype(jnp.bfloat16)
    update_pre = product(mesh_middle, weights[7]) + product(process_round, weights[8])
    update_hidden = jax.nn.silu(update_pre).astype(jnp.bfloat16)
    update_linear = product(update_hidden, weights[9])
    mesh_update = (mesh_middle.astype(jnp.float32) + layer_norm(update_linear)).astype(jnp.bfloat16)
    outer_cot = mesh_cotangent.astype(jnp.float32)
    cot_linear = layer_norm_back(update_linear, outer_cot).astype(jnp.bfloat16)
    grad_update_output = outer_sum(update_hidden, cot_linear)
    cot_update = (back_product(cot_linear, weights[9]) * swish_slope(update_pre)).astype(
        jnp.bfloat16
    )
    grad_update_self = outer_sum(mesh_middle, cot_update)
    grad_update_message = outer_sum(process_round, cot_update)
    cot_total = back_product(cot_update, weights[8])
    edge_cot = edge_cotangent.astype(jnp.float32)
    cot_edge = jnp.take(cot_total, mesh_target, axis=0) + edge_cot
    cot_plinear = layer_norm_back(process_linear, cot_edge).astype(jnp.bfloat16)
    grad_process_output = outer_sum(process_hidden, cot_plinear)
    cot_process = back_product(cot_plinear, weights[6]) * swish_slope(process_pre)
    cot_round = cot_process.astype(jnp.bfloat16)
    grad_process_edge = outer_sum(edge_latent, cot_round)
    edge_grad = (edge_cot + back_product(cot_round, weights[3])).astype(jnp.bfloat16)
    cot_receive = receive_sum(mesh_onehot, cot_process).astype(jnp.bfloat16)
    grad_process_receiver = outer_sum(mesh_middle, cot_receive)
    cot_slot = jax.ops.segment_sum(cot_process, mesh_slot, num_segments=mesh_source.shape[0])
    halo_partials = (
        cot_slot[mesh_rows : mesh_rows + halo_count].astype(jnp.bfloat16).reshape(4, -1, latent)
    )
    far_partials = (
        cot_slot[mesh_rows + halo_count :].astype(jnp.bfloat16).reshape(peer_count, -1, latent)
    )
    halo_returned = mesh_returns(halo_partials).astype(jnp.float32)
    far_returned = return_mesh(far_partials).reshape(-1, latent).astype(jnp.float32)
    sender_total = (
        cot_slot[:mesh_rows]
        + jax.ops.segment_sum(halo_returned, halo_table, num_segments=mesh_rows)
        + jax.ops.segment_sum(far_returned, far_table, num_segments=mesh_rows)
    )
    cot_sender = sender_total.astype(jnp.bfloat16)
    grad_process_sender = outer_sum(mesh_middle, cot_sender)
    cot_middle = (
        outer_cot
        + back_product(cot_update, weights[7])
        + back_product(cot_receive, weights[5])
        + back_product(cot_sender, weights[4])
    )
    process_grads = jnp.stack(
        [
            grad_process_edge,
            grad_process_sender,
            grad_process_receiver,
            grad_process_output,
            grad_update_self,
            grad_update_message,
            grad_update_output,
        ]
    )
    process_grads = lax.psum(process_grads, ("face", "sub"))
    cot_message = jnp.take(cot_middle, grid_target, axis=0)
    cot_elinear = layer_norm_back(encoder_linear, cot_message).astype(jnp.bfloat16)
    grad_encode_output = outer_sum(encoder_hidden, cot_elinear)
    cot_encoder = back_product(cot_elinear, weights[2]) * swish_slope(encoder_pre)
    cot_mesh_receive = receive_sum(grid_onehot, cot_encoder).astype(jnp.bfloat16)
    grad_encode_receiver = outer_sum(mesh_latent, cot_mesh_receive)
    mesh_grad = (cot_middle + back_product(cot_mesh_receive, weights[1])).astype(jnp.bfloat16)
    cot_gslot = jax.ops.segment_sum(cot_encoder, grid_slot, num_segments=grid_source.shape[0])
    grid_partials = cot_gslot[grid_rows:].astype(jnp.bfloat16).reshape(4, -1, latent)
    grid_returned = grid_returns(grid_partials).astype(jnp.float32)
    cot_grid = (
        cot_gslot[:grid_rows]
        + jax.ops.segment_sum(grid_returned, grid_table, num_segments=grid_rows)
    ).astype(jnp.bfloat16)
    grad_encode_sender = outer_sum(grid_latent, cot_grid)
    grid_grad = back_product(cot_grid, weights[0]).astype(jnp.bfloat16)
    encode_grads = jnp.stack([grad_encode_sender, grad_encode_receiver, grad_encode_output])
    encode_grads = lax.psum(encode_grads, ("face", "sub"))
    summed = jnp.concatenate([encode_grads, process_grads], axis=0)
    encode_scale = 1.0 / (grid_slot.shape[0] * peer_count) ** 0.5
    process_scale = 1.0 / (mesh_slot.shape[0] * peer_count) ** 0.5
    update_scale = 1.0 / (mesh_rows * peer_count) ** 0.5
    scale_column = jnp.array(
        [encode_scale] * 3 + [process_scale] * 4 + [update_scale] * 3, jnp.float32
    )
    weight_grads = (summed * scale_column[:, None, None]).astype(jnp.bfloat16)
    return (mesh_update, grid_grad, mesh_grad, edge_grad, weight_grads)


def solution(mesh):
    return jax.shard_map(
        on_device,
        mesh=mesh,
        in_specs=(
            P(("face", "sub"), None),
            P(("face", "sub"), None),
            P(("face", "sub"), None),
            P(("face", "sub"), None),
            P(("face", "sub"), None),
            P(("face", "sub"), None, None),
            P(("face", "sub")),
            P(("face", "sub")),
            P(("face", "sub"), None, None),
            P(("face", "sub"), None, None),
            P(("face", "sub")),
            P(("face", "sub")),
            P(),
        ),
        out_specs=(
            P(("face", "sub"), None),
            P(("face", "sub"), None),
            P(("face", "sub"), None),
            P(("face", "sub"), None),
            P(),
        ),
        check_vma=False,
    )
```

profile of v0, /device:TPU:0, one launch (start us, length us, event | category | flops | bytes accessed | tf_op | source)
XLA Modules:
  0.0 434.6 jit_solution(5734349062935372784)
XLA Ops:
  8.6 1.7 constant_dynamic-update-slice_fusion.4
  10.3 5.1 %gather_fusion.3 = bf16[1024,512]{1,0:T(8,128)(2,1)} fusion(bf16[512,512]{1,0:T(8,128)(2,1)S(1)} %get-tuple-element.43, s32[1024]{0:T(1024)S(1)} %fusion.116), kind=kCustom, calls=%fused_computation.clone | custom fusion | bytes 2101248 | tf_op jit(solution)/shard_map/jit(_take)/gather | solution.py:116
  15.4 1.5 broadcast_select_fusion
  17.9 2.4 collective-permute-start.3
  20.3 4.6 %collective-permute-start.1 = (bf16[256,512]{1,0:T(8,128)(2,1)}, bf16[256,512]{1,0:T(8,128)(2,1)}, u32[]{:S(2)}, u32[]{:S(2)}) collective-permute-start(bf16[256,512]{1,0:T(8,128)(2,1)} %get-tuple-element.31), channel_id=1, source_target_pairs={{0,7},{1,0},{2,1},{3,2},{4,3},{5,4},{6,5},{7,6},{8,15},{9,8},{10,9... | collective-permute-start | bytes 786440 | tf_op jit(solution)/shard_map/ppermute | solution.py:12
  31.7 1.3 pad_clamp_fusion
  34.5 2.3 copy.38
  36.7 4.9 %gather_fusion.4 = f32[1024,512]{1,0:T(8,128)} fusion(f32[128,512]{1,0:T(8,128)S(1)} %fusion.58, s32[1024]{0:T(1024)S(1)} %copy-done.50), kind=kCustom, calls=%fused_computation.1.clone | custom fusion | bytes 4198400 | tf_op jit(solution)/shard_map/jit(_take)/gather | solution.py:119
  43.7 5.1 %gather_fusion = bf16[1024,512]{1,0:T(8,128)(2,1)} fusion(bf16[1536,512]{1,0:T(8,128)(2,1)S(1)} %constant_dynamic-update-slice_fusion, s32[1024]{0:T(1024)S(1)} %copy-done.55), kind=kCustom, calls=%fused_computation.6 | custom fusion | bytes 2101248 | tf_op jit(solution)/shard_map/jit(_take)/gather | solution.py:119
  48.8 2.3 multiply_convert_fusion.3
  51.1 2.2 fusion.127
  55.9 2.0 fusion.52
  57.9 1.3 constant_dynamic-update-slice_fusion.10
  60.2 1.3 gather_fusion.1
  62.5 6.1 %all-to-all-start = ((bf16[32,4,512]{2,1,0:T(4,128)(2,1)}), bf16[32,4,512]{2,1,0:T(4,128)(2,1)S(1)}, u32[]{:S(2)}, u32[]{:S(2)}) async-start(bf16[32,4,512]{2,1,0:T(4,128)(2,1)} %broadcast_select_fusion.3), calls=%async_computation | async-start | bytes 262144 | tf_op jit(solution)/shard_map/all_to_all | solution.py:84
  68.7 1.5 collective-permute-start.7
  70.2 4.7 %collective-permute-start.5 = (bf16[64,512]{1,0:T(8,128)(2,1)S(1)}, bf16[64,512]{1,0:T(8,128)(2,1)S(1)}, u32[]{:S(2)}, u32[]{:S(2)}) collective-permute-start(bf16[64,512]{1,0:T(8,128)(2,1)S(1)} %get-tuple-element.40), channel_id=1, source_target_pairs={{0,7},{1,0},{2,1},{3,2},{4,3},{5,4},{6,5},{7,6},{8,15},{9,8},{10,9... | collective-permute-start | bytes 196616 | tf_op jit(solution)/shard_map/ppermute | solution.py:12
  74.9 4.9 %gather_fusion.6 = f32[1024,512]{1,0:T(8,128)} fusion(f32[128,512]{1,0:T(8,128)S(1)} %fusion.44, s32[1024]{0:T(1024)S(1)} %copy-done.52), kind=kCustom, calls=%fused_computation.3.clone | custom fusion | bytes 4198400 | tf_op jit(solution)/shard_map/jit(_take)/gather | solution.py:139
  80.0 4.0 gather_fusion.5
  84.0 4.1 multiply_convert_fusion.2
  88.2 2.2 fusion.128
  91.5 1.3 convolution_add_fusion.4
  92.9 1.5 fusion.129
  96.5 1.4 fusion.15
  97.9 1.4 fusion.37
  99.3 2.1 convolution_add_fusion.3
  101.4 5.1 %gather_fusion.7 = f32[1024,512]{1,0:T(8,128)} fusion(f32[128,512]{1,0:T(8,128)S(1)} %fusion.37, s32[1024]{0:T(1024)} %get-tuple-element.61), kind=kCustom, calls=%fused_computation.4.clone | custom fusion | bytes 4198400 | tf_op jit(solution)/shard_map/jit(_take)/gather | solution.py:160
  106.5 2.9 copy.37
  109.5 2.7 fusion.33
  115.2 4.0 fusion.130
  119.2 7.8 %scatter_custom_fusion = f32[512,512]{1,0:T(8,128)S(1)} fusion(s32[1024]{0:T(1024)} %param.28, f32[1024,512]{1,0:T(8,128)} %get-tuple-element.55, f32[]{:T(128)} %constant.90.clone.1), kind=kCustom, calls=%fused_computation.127 | custom fusion | flops 524288 | bytes 1049088 | tf_op jit(solution)/shard_map/scatter-add | solution.py:169
  128.6 1.8 fusion.14
  132.0 2.9 all-to-all-start.1
  135.0 4.8 %collective-permute-start.8 = (bf16[64,512]{1,0:T(8,128)(2,1)}, bf16[64,512]{1,0:T(8,128)(2,1)S(1)}, u32[]{:S(2)}, u32[]{:S(2)}) collective-permute-start(bf16[64,512]{1,0:T(8,128)(2,1)} %get-tuple-element.33), channel_id=1, source_target_pairs={{0,7},{1,0},{2,1},{3,2},{4,3},{5,4},{6,5},{7,6},{8,15},{9,8},{10,9... | collective-permute-start | bytes 196616 | tf_op jit(solution)/shard_map/ppermute | solution.py:12
  139.8 1.7 collective-permute-start.10
  141.5 1.3 convolution_add_fusion.2
  143.7 4.8 %collective-permute-done.9 = bf16[64,512]{1,0:T(8,128)(2,1)S(1)} collective-permute-done((bf16[64,512]{1,0:T(8,128)(2,1)S(1)}, bf16[64,512]{1,0:T(8,128)(2,1)S(1)}, u32[]{:S(2)}, u32[]{:S(2)}) %collective-permute-start.9) | collective-permute-done | bytes 65568 | tf_op jit(solution)/shard_map/ppermute | solution.py:12
  148.5 2.4 scatter_custom_fusion.1
  150.9 1.5 scatter_custom_fusion.2
  152.5 1.3 convolution_add_fusion.1
  153.9 4.9 %gather_fusion.8 = f32[1024,512]{1,0:T(8,128)} fusion(f32[128,512]{1,0:T(8,128)S(1)} %convolution_add_fusion.1, s32[1024]{0:T(1024)S(1)} %copy-done.51), kind=kCustom, calls=%fused_computation.5.clone | custom fusion | bytes 4198400 | tf_op jit(solution)/shard_map/jit(_take)/gather | solution.py:203
  158.8 3.1 copy.40
  161.9 2.3 select_reduce_fusion
  166.0 2.7 multiply_multiply_fusion
  168.8 1.7 convolution_bitcast_fusion.1
  171.0 8.5 %scatter_custom_fusion.3 = f32[1536,512]{1,0:T(8,128)} fusion(s32[1024]{0:T(1024)} %param.24, f32[1024,512]{1,0:T(8,128)S(1)} %multiply_multiply_fusion, f32[]{:T(128)} %constant.90.clone.1), kind=kCustom, calls=%fused_computation.43 | custom fusion | flops 524288 | bytes 3146240 | tf_op jit(solution)/shard_map/scatter-add | solution.py:210
  179.5 2.1 convert.9
  183.1 1.7 collective-permute-start.14
  184.8 2.2 collective-permute-start.13
  187.0 1.3 fusion.13
  188.3 1.3 fusion.12
  189.6 1.7 fusion.8
  191.4 1.3 fusion.11
  192.7 1.3 fusion.10
  194.1 1.5 fusion.9
  197.1 8.2 %scatter_custom_fusion.4 = f32[512,512]{1,0:T(8,128)S(1)} fusion(f32[512,512]{1,0:T(8,128)S(1)} %slice-done, s32[1024]{0:T(1024)} %bitcast.150, bf16[256,512]{1,0:T(8,128)(2,1)} %copy-done.36, bf16[]{:T(256)} %constant.108, bf16[256,512]{1,0:T(8,128)(2,1)} %copy-done.37, bf16[256,512]{1,0:T(8,128)(2,1)} %collective-permute-done.13, ...), kind=kCustom, calls=%fused_computation.23 | custom fusion | flops 4718592 | bytes 2097664 | tf_op jit(solution)/shard_map/scatter-add | solution.py:215
  205.8 3.2 pad_maximum_fusion
  210.2 3.1 fusion.1
  213.3 2.5 copy.49
  215.8 2.0 fusion.16
  217.9 2.3 convolution_convert_fusion
  220.2 191.5 %all-reduce.3.cloned.1.call-done = (f32[7,512,512]{1,2,0:T(8,128)}, f32[3,512,512]{1,2,0:T(8,128)}) async-done(((f32[7,512,512]{1,2,0:T(8,128)}, f32[3,512,512]{1,2,0:T(8,128)}), (f32[7,512,512]{1,2,0:T(8,128)}, f32[3,512,512]{1,2,0:T(8,128)})) %all-reduce.3.cloned.1.call-update) | async-done | bytes 10485776 | tf_op jit(solution)/shard_map/psum | solution.py:202
  411.7 7.9 %fusion = bf16[10,512,512]{1,2,0:T(8,128)(2,1)} fusion(f32[7,512,512]{1,2,0:T(8,128)} %get-tuple-element.23, f32[3,512,512]{1,2,0:T(8,128)} %get-tuple-element.24, f32[10]{0:T(128)S(1)} %copy-done.71), kind=kLoop, calls=%fused_computation.15 | loop fusion | flops 7864320 | bytes 15728680 | tf_op jit(solution)/shard_map/convert_element_type | solution.py:228
  419.6 8.0 %copy.50 = bf16[10,512,512]{2,1,0:T(8,128)(2,1)} copy(bf16[10,512,512]{1,2,0:T(8,128)(2,1)} %fusion) | data formatting | bytes 10485760
  (259 shorter events, 34.6 us)
Async XLA Ops:
  7.2 76.8 %copy-start = (bf16[1024,512]{1,0:T(8,128)(2,1)S(1)}, bf16[1024,512]{1,0:T(8,128)(2,1)}, u32[]{:S(2)}) copy-start(bf16[1024,512]{1,0:T(8,128)(2,1)} %param.20) | copy-start | bytes 3145732
  15.4 9.5 %copy-start.63 = (s32[1,4,64]{2,1,0:T(4,128)S(1)}, s32[1,4,64]{2,1,0:T(4,128)}, u32[]{:S(2)}) copy-start(s32[1,4,64]{2,1,0:T(4,128)} %param.26) | copy-start | bytes 3076
  15.4 9.7 %copy-start.40 = (s32[1024]{0:T(1024)S(1)}, s32[1024]{0:T(1024)}, u32[]{:S(2)}) copy-start(s32[1024]{0:T(1024)} %param.25) | copy-start | bytes 12292
  15.4 9.7 %copy-start.57 = (s32[1024]{0:T(1024)S(1)}, s32[1024]{0:T(1024)}, u32[]{:S(2)}) copy-start(s32[1024]{0:T(1024)} %param.24) | copy-start | bytes 12292
  15.4 10.9 %copy-start.42 = (s32[1024]{0:T(1024)S(1)}, s32[1024]{0:T(1024)}, u32[]{:S(2)}) copy-start(s32[1024]{0:T(1024)} %param.29) | copy-start | bytes 12292
  15.4 10.9 %copy-start.56 = (s32[1024]{0:T(1024)S(1)}, s32[1024]{0:T(1024)}, u32[]{:S(2)}) copy-start(s32[1024]{0:T(1024)} %param.28) | copy-start | bytes 12292
  15.4 12.0 %copy-start.62 = (s32[1,32,4]{1,2,0:T(4,128)S(1)}, s32[1,32,4]{1,2,0:T(4,128)}, u32[]{:S(2)}) copy-start(s32[1,32,4]{1,2,0:T(4,128)} %param.27) | copy-start | bytes 1540
  15.4 14.4 %copy-start.18 = (bf16[128,512]{1,0:T(8,128)(2,1)S(1)}, bf16[128,512]{1,0:T(8,128)(2,1)}, u32[]{:S(2)}) copy-start(bf16[128,512]{1,0:T(8,128)(2,1)} %param.19) | copy-start | bytes 393220
  17.9 25.7 %collective-permute-start.3 = (bf16[256,512]{1,0:T(8,128)(2,1)}, bf16[256,512]{1,0:T(8,128)(2,1)S(1)}, u32[]{:S(2)}, u32[]{:S(2)}) collective-permute-start(bf16[256,512]{1,0:T(8,128)(2,1)} %get-tuple-element.29), channel_id=1, source_target_pairs={{0,24},{8,0},{16,8},{24,16},{1,25},{9,1},{17,9},{25,17},{2,26},{10... | collective-permute-start | bytes 786440 | tf_op jit(solution)/shard_map/ppermute | solution.py:12
  20.3 23.3 %collective-permute-start.2 = (bf16[256,512]{1,0:T(8,128)(2,1)}, bf16[256,512]{1,0:T(8,128)(2,1)S(1)}, u32[]{:S(2)}, u32[]{:S(2)}) collective-permute-start(bf16[256,512]{1,0:T(8,128)(2,1)} %get-tuple-element.30), channel_id=1, source_target_pairs={{0,8},{8,16},{16,24},{24,0},{1,9},{9,17},{17,25},{25,1},{2,10},{10... | collective-permute-start | bytes 786440 | tf_op jit(solution)/shard_map/ppermute | solution.py:12
  20.3 22.3 %collective-permute-start.1 = (bf16[256,512]{1,0:T(8,128)(2,1)}, bf16[256,512]{1,0:T(8,128)(2,1)}, u32[]{:S(2)}, u32[]{:S(2)}) collective-permute-start(bf16[256,512]{1,0:T(8,128)(2,1)} %get-tuple-element.31), channel_id=1, source_target_pairs={{0,7},{1,0},{2,1},{3,2},{4,3},{5,4},{6,5},{7,6},{8,15},{9,8},{10,9... | collective-permute-start | bytes 786440 | tf_op jit(solution)/shard_map/ppermute | solution.py:12
  24.9 16.7 %collective-permute-start = (bf16[256,512]{1,0:T(8,128)(2,1)}, bf16[256,512]{1,0:T(8,128)(2,1)}, u32[]{:S(2)}, u32[]{:S(2)}) collective-permute-start(bf16[256,512]{1,0:T(8,128)(2,1)} %get-tuple-element.32), channel_id=1, source_target_pairs={{0,1},{1,2},{2,3},{3,4},{4,5},{5,6},{6,7},{7,0},{8,9},{9,10},{10,1... | collective-permute-start | bytes 786440 | tf_op jit(solution)/shard_map/ppermute | solution.py:12
  24.9 4.2 copy-start.68
  33.7 3.1 copy-start.50
  43.7 5.1 %copy-start.58 = (pred[1024]{0:T(1024)(128)(4,1)S(1)}, pred[1024]{0:T(1024)(128)(4,1)}, u32[]{:S(2)}) copy-start(pred[1024]{0:T(1024)(128)(4,1)} %get-tuple-element.62) | copy-start | bytes 3076
  43.7 5.1 %copy-start.64 = (pred[1024]{0:T(1024)(128)(4,1)S(1)}, pred[1024]{0:T(1024)(128)(4,1)}, u32[]{:S(2)}) copy-start(pred[1024]{0:T(1024)(128)(4,1)} %get-tuple-element.63) | copy-start | bytes 3076
  53.7 4.3 copy-start.46
  60.2 14.8 %copy-start.52 = (s32[1024]{0:T(1024)S(1)}, s32[1024]{0:T(1024)}, u32[]{:S(2)}) copy-start(s32[1024]{0:T(1024)} %get-tuple-element.61) | copy-start | bytes 12292
  61.7 18.2 %collective-permute-start.4 = (bf16[64,512]{1,0:T(8,128)(2,1)S(1)}, bf16[64,512]{1,0:T(8,128)(2,1)S(1)}, u32[]{:S(2)}, u32[]{:S(2)}) collective-permute-start(bf16[64,512]{1,0:T(8,128)(2,1)S(1)} %get-tuple-element.41), channel_id=1, source_target_pairs={{0,1},{1,2},{2,3},{3,4},{4,5},{5,6},{6,7},{7,0},{8,9},{9,10},{10,1... | collective-permute-start | bytes 196616 | tf_op jit(solution)/shard_map/ppermute | solution.py:12
  62.5 17.4 %all-to-all-start = ((bf16[32,4,512]{2,1,0:T(4,128)(2,1)}), bf16[32,4,512]{2,1,0:T(4,128)(2,1)S(1)}, u32[]{:S(2)}, u32[]{:S(2)}) async-start(bf16[32,4,512]{2,1,0:T(4,128)(2,1)} %broadcast_select_fusion.3), calls=%async_computation | async-start | bytes 262144 | tf_op jit(solution)/shard_map/all_to_all | solution.py:84
  68.7 11.2 %collective-permute-start.7 = (bf16[64,512]{1,0:T(8,128)(2,1)S(1)}, bf16[64,512]{1,0:T(8,128)(2,1)S(1)}, u32[]{:S(2)}, u32[]{:S(2)}) collective-permute-start(bf16[64,512]{1,0:T(8,128)(2,1)S(1)} %get-tuple-element.38), channel_id=1, source_target_pairs={{0,24},{8,0},{16,8},{24,16},{1,25},{9,1},{17,9},{25,17},{2,26},{10... | collective-permute-start | bytes 196616 | tf_op jit(solution)/shard_map/ppermute | solution.py:12
  70.2 9.6 %collective-permute-start.6 = (bf16[64,512]{1,0:T(8,128)(2,1)S(1)}, bf16[64,512]{1,0:T(8,128)(2,1)S(1)}, u32[]{:S(2)}, u32[]{:S(2)}) collective-permute-start(bf16[64,512]{1,0:T(8,128)(2,1)S(1)} %get-tuple-element.39), channel_id=1, source_target_pairs={{0,8},{8,16},{16,24},{24,0},{1,9},{9,17},{17,25},{25,1},{2,10},{10... | collective-permute-start | bytes 196616 | tf_op jit(solution)/shard_map/ppermute | solution.py:12
  70.2 9.6 %collective-permute-start.5 = (bf16[64,512]{1,0:T(8,128)(2,1)S(1)}, bf16[64,512]{1,0:T(8,128)(2,1)S(1)}, u32[]{:S(2)}, u32[]{:S(2)}) collective-permute-start(bf16[64,512]{1,0:T(8,128)(2,1)S(1)} %get-tuple-element.40), channel_id=1, source_target_pairs={{0,7},{1,0},{2,1},{3,2},{4,3},{5,4},{6,5},{7,6},{8,15},{9,8},{10,9... | collective-permute-start | bytes 196616 | tf_op jit(solution)/shard_map/ppermute | solution.py:12
  74.9 5.0 %copy-start.54 = (s32[1024]{0:T(1024)S(1)}, s32[1024]{0:T(1024)}, u32[]{:S(2)}) copy-start(s32[1024]{0:T(1024)} %get-tuple-element.60) | copy-start | bytes 12292
  80.0 4.0 copy-start.60
  80.0 4.0 copy-start.69
  84.0 4.2 copy-start.22
  90.7 3.6 copy-start.48
  91.5 3.9 copy-start.20
  91.5 3.1 copy-start.33
  92.8 5.1 %copy-start.38 = (f32[128,512]{1,0:T(8,128)}, f32[128,512]{1,0:T(8,128)S(1)}, u32[]{:S(2)}) copy-start(f32[128,512]{1,0:T(8,128)S(1)} %convolution_add_fusion.4) | copy-start | bytes 786436
  94.3 5.0 %copy-start.24 = (f32[128,512]{1,0:T(8,128)}, f32[128,512]{1,0:T(8,128)S(1)}, u32[]{:S(2)}) copy-start(f32[128,512]{1,0:T(8,128)S(1)} %get-tuple-element.53) | copy-start | bytes 786436
  106.5 2.9 copy-start.49
  106.5 2.9 copy-start.61
  109.5 2.8 copy-start.6
  112.3 2.9 copy-start.79
  113.0 6.2 %copy-start.29 = (bf16[1024,512]{0,1:T(8,128)(2,1)}, bf16[1024,512]{0,1:T(8,128)(2,1)S(1)}, u32[]{:S(2)}) copy-start(bf16[1024,512]{0,1:T(8,128)(2,1)S(1)} %multiply_convert_fusion.1) | copy-start | bytes 3145732
  119.2 11.1 %copy-start.10 = (bf16[1024,512]{1,0:T(8,128)(2,1)}, bf16[1024,512]{1,0:T(8,128)(2,1)S(1)}, u32[]{:S(2)}) copy-start(bf16[1024,512]{1,0:T(8,128)(2,1)S(1)} %get-tuple-element.54) | copy-start | bytes 3145732
  130.4 9.4 %copy-start.45 = (bf16[64,512]{1,0:T(8,128)(2,1)S(1)}, bf16[64,512]{1,0:T(8,128)(2,1)}, u32[]{:S(2)}) copy-start(bf16[64,512]{1,0:T(8,128)(2,1)} %get-tuple-element.35) | copy-start | bytes 196612
  130.4 11.1 %copy-start.44 = (bf16[64,512]{1,0:T(8,128)(2,1)S(1)}, bf16[64,512]{1,0:T(8,128)(2,1)}, u32[]{:S(2)}) copy-start(bf16[64,512]{1,0:T(8,128)(2,1)} %get-tuple-element.36) | copy-start | bytes 196612
  130.4 11.1 %copy-start.31 = (f32[128,512]{1,0:T(8,128)S(1)}, f32[128,512]{1,0:T(8,128)}, u32[]{:S(2)}) copy-start(f32[128,512]{1,0:T(8,128)} %convolution_add_fusion.3) | copy-start | bytes 786436
  132.0 18.9 %all-to-all-start.1 = ((bf16[32,4,512]{2,1,0:T(4,128)(2,1)}), bf16[32,4,512]{2,1,0:T(4,128)(2,1)S(1)}, u32[]{:S(2)}, u32[]{:S(2)}) async-start(bf16[32,4,512]{2,1,0:T(4,128)(2,1)} %reshape.209), calls=%async_computation.1 | async-start | bytes 262144 | tf_op jit(solution)/shard_map/all_to_all | solution.py:88
  134.9 276.8 %all-reduce.3.cloned.1.call-start = ((), (), s32[]{:S(2)}) async-start(), calls=%async_computation.2 | async-start | bytes 20971520 | tf_op jit(solution)/shard_map/psum | solution.py:202
  135.0 7.9 %collective-permute-start.8 = (bf16[64,512]{1,0:T(8,128)(2,1)}, bf16[64,512]{1,0:T(8,128)(2,1)S(1)}, u32[]{:S(2)}, u32[]{:S(2)}) collective-permute-start(bf16[64,512]{1,0:T(8,128)(2,1)} %get-tuple-element.33), channel_id=1, source_target_pairs={{0,7},{1,0},{2,1},{3,2},{4,3},{5,4},{6,5},{7,6},{8,15},{9,8},{10,9... | collective-permute-start | bytes 196616 | tf_op jit(solution)/shard_map/ppermute | solution.py:12
  139.8 3.9 collective-permute-start.11
  139.8 3.9 collective-permute-start.10
  141.5 12.3 %copy-start.51 = (s32[1024]{0:T(1024)S(1)}, s32[1024]{0:T(1024)}, u32[]{:S(2)}) copy-start(s32[1024]{0:T(1024)} %get-tuple-element.59) | copy-start | bytes 12292
  141.5 7.0 %collective-permute-start.9 = (bf16[64,512]{1,0:T(8,128)(2,1)S(1)}, bf16[64,512]{1,0:T(8,128)(2,1)S(1)}, u32[]{:S(2)}, u32[]{:S(2)}) collective-permute-start(bf16[64,512]{1,0:T(8,128)(2,1)S(1)} %copy-done.44), channel_id=1, source_target_pairs={{0,1},{1,2},{2,3},{3,4},{4,5},{5,6},{6,7},{7,0},{8,9},{9,10},{10,1... | collective-permute-start | bytes 196616 | tf_op jit(solution)/shard_map/ppermute | solution.py:12
  158.8 3.1 copy-start.3
  158.8 3.1 copy-start.47
  158.8 3.1 copy-start.59
  182.9 6.8 %copy-start.28 = (bf16[1024,512]{1,0:T(8,128)(2,1)S(1)}, bf16[1024,512]{1,0:T(8,128)(2,1)}, u32[]{:S(2)}) copy-start(bf16[1024,512]{1,0:T(8,128)(2,1)} %copy-done.27) | copy-start | bytes 3145732
  182.9 6.8 %copy-start.30 = (bf16[1024,512]{0,1:T(8,128)(2,1)S(1)}, bf16[1024,512]{0,1:T(8,128)(2,1)}, u32[]{:S(2)}) copy-start(bf16[1024,512]{0,1:T(8,128)(2,1)} %copy-done.29) | copy-start | bytes 3145732
  183.0 12.6 %collective-permute-start.12 = (bf16[256,512]{1,0:T(8,128)(2,1)S(1)}, bf16[256,512]{1,0:T(8,128)(2,1)S(1)}, u32[]{:S(2)}, u32[]{:S(2)}) collective-permute-start(bf16[256,512]{1,0:T(8,128)(2,1)S(1)} %get-tuple-element.25), channel_id=1, source_target_pairs={{0,7},{1,0},{2,1},{3,2},{4,3},{5,4},{6,5},{7,6},{8,15},{9,8},{10,9... | collective-permute-start | bytes 786440 | tf_op jit(solution)/shard_map/ppermute | solution.py:12
  183.0 12.6 %collective-permute-start.15 = (bf16[256,512]{1,0:T(8,128)(2,1)S(1)}, bf16[256,512]{1,0:T(8,128)(2,1)S(1)}, u32[]{:S(2)}, u32[]{:S(2)}) collective-permute-start(bf16[256,512]{1,0:T(8,128)(2,1)S(1)} %get-tuple-element.26), channel_id=1, source_target_pairs={{0,8},{8,16},{16,24},{24,0},{1,9},{9,17},{17,25},{25,1},{2,10},{10... | collective-permute-start | bytes 786440 | tf_op jit(solution)/shard_map/ppermute | solution.py:12
  183.1 12.5 %collective-permute-start.14 = (bf16[256,512]{1,0:T(8,128)(2,1)S(1)}, bf16[256,512]{1,0:T(8,128)(2,1)S(1)}, u32[]{:S(2)}, u32[]{:S(2)}) collective-permute-start(bf16[256,512]{1,0:T(8,128)(2,1)S(1)} %get-tuple-element.27), channel_id=1, source_target_pairs={{0,24},{8,0},{16,8},{24,16},{1,25},{9,1},{17,9},{25,17},{2,26},{10... | collective-permute-start | bytes 786440 | tf_op jit(solution)/shard_map/ppermute | solution.py:12
  184.8 12.3 %collective-permute-start.13 = (bf16[256,512]{1,0:T(8,128)(2,1)S(1)}, bf16[256,512]{1,0:T(8,128)(2,1)}, u32[]{:S(2)}, u32[]{:S(2)}) collective-permute-start(bf16[256,512]{1,0:T(8,128)(2,1)S(1)} %get-tuple-element.28), channel_id=1, source_target_pairs={{0,1},{1,2},{2,3},{3,4},{4,5},{5,6},{6,7},{7,0},{8,9},{9,10},{10,1... | collective-permute-start | bytes 786440 | tf_op jit(solution)/shard_map/ppermute | solution.py:12
  188.3 3.0 copy-start.16
  189.6 3.1 copy-start.21
  191.3 2.8 copy-start.39
  191.4 5.7 %slice-start = ((f32[1536,512]{1,0:T(8,128)}), f32[512,512]{1,0:T(8,128)S(1)}, s32[]{:S(2)}) async-start(f32[1536,512]{1,0:T(8,128)} %scatter_custom_fusion.3), calls=%async_computation.3 | async-start | bytes 2097152 | tf_op jit(solution)/shard_map/slice | solution.py:214
  195.6 9.7 %copy-start.32 = (bf16[512,512]{1,0:T(8,128)(2,1)S(1)}, bf16[512,512]{1,0:T(8,128)(2,1)}, u32[]{:S(2)}) copy-start(bf16[512,512]{1,0:T(8,128)(2,1)} %param.18) | copy-start | bytes 1572868
  215.8 195.9 %copy-start.71 = (f32[10]{0:T(128)S(1)}, f32[10]{0:T(128)}, u32[]{:S(2)}) copy-start(f32[10]{0:T(128)} %constant.95.clone) | copy-start | bytes 124
  419.6 8.0 %copy-start.1 = (bf16[1024,512]{1,0:T(8,128)(2,1)S(1)}, bf16[1024,512]{1,0:T(8,128)(2,1)}, u32[]{:S(2)}) copy-start(bf16[1024,512]{1,0:T(8,128)(2,1)} %param.20) | copy-start | bytes 3145732
  (37 other events, 65.6 us)
Sparse Core Ops, SparseCore 0:
  209.1 202.4 all-reduce.2
where the time goes:
time: 442 us; the launch traced here: 435 us
  waiting for transfers between devices  197 us (45%)
  local copies, waits for them, and re-layouts  71.8 us (16%)
  other arithmetic  60.3 us (14%)
  matrix products  57 us (13%)
  starting transfers between devices  32.9 us (7%)
  between operations  15.4 us (3%)
    psum x1, waiting for transfers between devices, on_device(): process_grads = lax.psum(process_grads, ('face', 'sub'))  192 us
    unnamed x172, local copies, waits for them, and re-layouts  24.5 us
    ppermute x16, starting transfers between devices, shifted(): return lax.ppermute(value, axis, pairs)  23.8 us
    dot_general x10, matrix products, back_product(): lax.dot_general(former, latter, (((1,), (1,)), ((), ())), preferred_eleme...  21.7 us
    dot_general x10, matrix products, product(): return jnp.dot(former, latter, preferred_element_type=jnp.float32)  18.8 us
    dot_general x16, matrix products, outer_sum(): lax.dot_general(former, latter, (((0,), (0,)), ((), ())), preferred_eleme...  16.5 us
  transfers between devices with their start and end apart: 19, of which 3 were waited for; matrix products, arithmetic and copies ran while one was open for 11% of the time, Pallas kernels for 0%

commit v1 on v0

--- a/solution.py
+++ b/solution.py
@@ -199,7 +199,7 @@
             grad_update_output,
         ]
     )
-    process_grads = lax.psum(process_grads, ("face", "sub"))
+    process_grads = lax.psum(lax.psum(process_grads, "sub"), "face")
     cot_message = jnp.take(cot_middle, grid_target, axis=0)
     cot_elinear = layer_norm_back(encoder_linear, cot_message).astype(jnp.bfloat16)
     grad_encode_output = outer_sum(encoder_hidden, cot_elinear)

time: 442 us -> 711 us (1.61)
  waiting for transfers between devices: 197 us -> 466 us
    psum x1 -> x3, waiting for transfers between devices: 192 us -> 452 us  [the longest x2 320 us: on_device(): process_grads = lax.psum(lax.psum(process_grads, 'sub'), 'face')]
    ppermute x16, waiting for transfers between devices: 5.59 us -> 14.1 us  [shifted(): return lax.ppermute(value, axis, pairs)]
    unnamed x172 -> x174, local copies, waits for them, and re-layouts: 24.5 us -> 27.5 us
  transfers between devices with their start and end apart: 19 -> 21, of which waited for: 3 -> 8; matrix products, arithmetic and copies ran while one was open for 11% -> 11% of each run, Pallas kernels for 0% -> 0%
where the time goes in v1:
time: 711 us; the launch traced here: 704 us
  waiting for transfers between devices  466 us (66%)
  local copies, waits for them, and re-layouts  74.5 us (10%)
  other arithmetic  59.6 us (8%)
  matrix products  56.2 us (8%)
  starting transfers between devices  32.8 us (5%)
  between operations  15.1 us (2%)
    psum x2, waiting for transfers between devices, on_device(): process_grads = lax.psum(lax.psum(process_grads, 'sub'), 'face')  320 us
    psum x1, waiting for transfers between devices, on_device(): encode_grads = lax.psum(encode_grads, ('face', 'sub'))  132 us
    unnamed x174, local copies, waits for them, and re-layouts  27.5 us
    ppermute x16, starting transfers between devices, shifted(): return lax.ppermute(value, axis, pairs)  23.6 us
    dot_general x10, matrix products, back_product(): lax.dot_general(former, latter, (((1,), (1,)), ((), ())), preferred_eleme...  20.9 us
    dot_general x10, matrix products, product(): return jnp.dot(former, latter, preferred_element_type=jnp.float32)  18.7 us
    dot_general x16, matrix products, outer_sum(): lax.dot_general(former, latter, (((0,), (0,)), ((), ())), preferred_eleme...  16.6 us
  transfers between devices with their start and end apart: 21, of which 8 were waited for; matrix products, arithmetic and copies ran while one was open for 11% of the time, Pallas kernels for 0%

profile of v1, /device:TPU:0, one launch (start us, length us, event | category | flops | bytes accessed | tf_op | source)
XLA Modules:
  0.0 704.2 jit_solution(4994659283480988015)
XLA Ops:
  8.6 1.6 constant_dynamic-update-slice_fusion.4
  10.2 5.1 gather_fusion.3
  15.3 1.5 broadcast_select_fusion
  17.8 2.4 collective-permute-start.3
  20.2 4.6 collective-permute-start.1
  34.4 2.3 copy.38
  36.7 4.9 gather_fusion.4
  43.6 5.1 gather_fusion
  48.7 2.3 multiply_convert_fusion.3
  51.0 2.2 fusion.127
  55.8 2.0 fusion.52
  62.4 6.1 all-to-all-start
  68.5 1.5 collective-permute-start.7
  70.1 4.7 collective-permute-start.5
  74.8 4.9 gather_fusion.6
  79.9 4.0 gather_fusion.5
  83.9 4.1 multiply_convert_fusion.2
  88.0 2.2 fusion.128
  91.9 1.3 convolution_add_fusion.4
  93.3 1.5 fusion.129
  95.8 1.4 fusion.15
  97.9 1.3 fusion.37
  99.2 5.2 gather_fusion.7
  104.4 2.9 copy.37
  107.3 2.7 fusion.33
  113.0 4.0 fusion.130
  117.1 7.8 %scatter_custom_fusion = f32[512,512]{1,0:T(8,128)S(1)} fusion(s32[1024]{0:T(1024)} %param.28, f32[1024,512]{1,0:T(8,128)} %get-tuple-element.53, f32[]{:T(128)} %constant.90.clone.1), kind=kCustom, calls=%fused_computation.127 | custom fusion | flops 524288 | bytes 1049088 | tf_op jit(solution)/shard_map/scatter-add | solution.py:169
  127.9 3.0 all-to-all-start.1
  130.9 4.6 collective-permute-start.8
  135.5 1.7 collective-permute-start.10
  137.4 1.8 fusion.14
  140.6 4.0 collective-permute-done.9
  144.7 2.7 scatter_custom_fusion.1
  147.4 1.7 scatter_custom_fusion.2
  150.4 1.3 fusion.12
  151.7 1.7 fusion.8
  153.5 1.4 fusion.11
  154.9 1.3 fusion.10
  156.2 1.5 fusion.9
  157.8 1.3 convolution_add_fusion.3
  159.2 1.3 convolution_add_fusion.2
  160.5 1.4 convolution_add_fusion.1
  162.0 4.9 gather_fusion.8
  166.8 3.1 copy.40
  169.9 2.3 select_reduce_fusion
  174.4 2.6 multiply_multiply_fusion
  177.1 8.7 %scatter_custom_fusion.3 = f32[1536,512]{1,0:T(8,128)} fusion(s32[1024]{0:T(1024)} %param.24, f32[1024,512]{1,0:T(8,128)S(1)} %multiply_multiply_fusion, f32[]{:T(128)} %constant.90.clone.1), kind=kCustom, calls=%fused_computation.43 | custom fusion | flops 524288 | bytes 3146240 | tf_op jit(solution)/shard_map/scatter-add | solution.py:210
  185.8 2.1 convert.9
  188.5 1.7 collective-permute-start.14
  190.2 1.6 collective-permute-start.13
  194.5 1.7 convolution_bitcast_fusion.1
  196.2 4.2 collective-permute-done.12
  201.8 5.7 collective-permute-done.13
  207.5 8.1 %scatter_custom_fusion.4 = f32[512,512]{1,0:T(8,128)S(1)} fusion(f32[512,512]{1,0:T(8,128)S(1)} %slice-done, s32[1024]{0:T(1024)} %bitcast.150, bf16[256,512]{1,0:T(8,128)(2,1)} %copy-done.36, bf16[]{:T(256)} %constant.108, bf16[256,512]{1,0:T(8,128)(2,1)} %copy-done.37, bf16[256,512]{1,0:T(8,128)(2,1)} %collective-permute-done.13, ...), kind=kCustom, calls=%fused_computation.23 | custom fusion | flops 4718592 | bytes 2097664 | tf_op jit(solution)/shard_map/scatter-add | solution.py:215
  216.9 2.0 pad_maximum_fusion
  218.9 182.0 %all-reduce.6.cloned.1.call-done = f32[7,512,512]{1,2,0:T(8,128)} async-done(((f32[7,512,512]{1,2,0:T(8,128)}), f32[7,512,512]{1,2,0:T(8,128)}) %all-reduce.6.cloned.1.call-update) | async-done | bytes 7340048 | tf_op jit(solution)/shard_map/psum | solution.py:202
  402.1 3.1 fusion.1
  405.2 2.3 copy.49
  407.5 2.0 fusion.16
  409.5 2.3 convolution_convert_fusion
  411.8 132.0 %all-reduce.4.cloned.1.call-done = f32[3,512,512]{1,2,0:T(8,128)} async-done(((f32[3,512,512]{1,2,0:T(8,128)}), f32[3,512,512]{1,2,0:T(8,128)}) %all-reduce.4.cloned.1.call-update) | async-done | bytes 3145744 | tf_op jit(solution)/shard_map/psum | solution.py:220
  543.8 137.8 %all-reduce.8.cloned.1.call-done = f32[7,512,512]{1,2,0:T(8,128)} async-done(((f32[7,512,512]{1,2,0:T(8,128)}), f32[7,512,512]{1,2,0:T(8,128)}) %all-reduce.8.cloned.1.call-update) | async-done | bytes 7340048 | tf_op jit(solution)/shard_map/psum | solution.py:202
  681.5 7.9 %fusion = bf16[10,512,512]{1,2,0:T(8,128)(2,1)} fusion(f32[7,512,512]{1,2,0:T(8,128)} %all-reduce.8.cloned.1.call-done, f32[3,512,512]{1,2,0:T(8,128)} %all-reduce.4.cloned.1.call-done, f32[10]{0:T(128)S(1)} %copy-done.72), kind=kLoop, calls=%fused_computation.15 | loop fusion | flops 7864320 | bytes 15728680 | tf_op jit(solution)/shard_map/convert_element_type | solution.py:228
  689.4 8.0 %copy.50 = bf16[10,512,512]{2,1,0:T(8,128)(2,1)} copy(bf16[10,512,512]{1,2,0:T(8,128)(2,1)} %fusion) | data formatting | bytes 10485760
  (266 shorter events, 42.9 us)
Async XLA Ops:
  7.2 76.7 %copy-start = (bf16[1024,512]{1,0:T(8,128)(2,1)S(1)}, bf16[1024,512]{1,0:T(8,128)(2,1)}, u32[]{:S(2)}) copy-start(bf16[1024,512]{1,0:T(8,128)(2,1)} %param.20) | copy-start | bytes 3145732
  15.3 9.5 %copy-start.64 = (s32[1,4,64]{2,1,0:T(4,128)S(1)}, s32[1,4,64]{2,1,0:T(4,128)}, u32[]{:S(2)}) copy-start(s32[1,4,64]{2,1,0:T(4,128)} %param.26) | copy-start | bytes 3076
  15.3 9.7 %copy-start.40 = (s32[1024]{0:T(1024)S(1)}, s32[1024]{0:T(1024)}, u32[]{:S(2)}) copy-start(s32[1024]{0:T(1024)} %param.25) | copy-start | bytes 12292
  15.3 9.7 %copy-start.58 = (s32[1024]{0:T(1024)S(1)}, s32[1024]{0:T(1024)}, u32[]{:S(2)}) copy-start(s32[1024]{0:T(1024)} %param.24) | copy-start | bytes 12292
  15.3 10.9 %copy-start.42 = (s32[1024]{0:T(1024)S(1)}, s32[1024]{0:T(1024)}, u32[]{:S(2)}) copy-start(s32[1024]{0:T(1024)} %param.29) | copy-start | bytes 12292
  15.3 10.9 %copy-start.57 = (s32[1024]{0:T(1024)S(1)}, s32[1024]{0:T(1024)}, u32[]{:S(2)}) copy-start(s32[1024]{0:T(1024)} %param.28) | copy-start | bytes 12292
  15.3 12.1 %copy-start.63 = (s32[1,32,4]{1,2,0:T(4,128)S(1)}, s32[1,32,4]{1,2,0:T(4,128)}, u32[]{:S(2)}) copy-start(s32[1,32,4]{1,2,0:T(4,128)} %param.27) | copy-start | bytes 1540
  15.3 14.5 %copy-start.17 = (bf16[128,512]{1,0:T(8,128)(2,1)S(1)}, bf16[128,512]{1,0:T(8,128)(2,1)}, u32[]{:S(2)}) copy-start(bf16[128,512]{1,0:T(8,128)(2,1)} %param.19) | copy-start | bytes 393220
  17.8 25.7 %collective-permute-start.3 = (bf16[256,512]{1,0:T(8,128)(2,1)}, bf16[256,512]{1,0:T(8,128)(2,1)S(1)}, u32[]{:S(2)}, u32[]{:S(2)}) collective-permute-start(bf16[256,512]{1,0:T(8,128)(2,1)} %get-tuple-element.27), channel_id=1, source_target_pairs={{0,24},{8,0},{16,8},{24,16},{1,25},{9,1},{17,9},{25,17},{2,26},{10... | collective-permute-start | bytes 786440 | tf_op jit(solution)/shard_map/ppermute | solution.py:12
  20.2 23.3 %collective-permute-start.2 = (bf16[256,512]{1,0:T(8,128)(2,1)}, bf16[256,512]{1,0:T(8,128)(2,1)S(1)}, u32[]{:S(2)}, u32[]{:S(2)}) collective-permute-start(bf16[256,512]{1,0:T(8,128)(2,1)} %get-tuple-element.28), channel_id=1, source_target_pairs={{0,8},{8,16},{16,24},{24,0},{1,9},{9,17},{17,25},{25,1},{2,10},{10... | collective-permute-start | bytes 786440 | tf_op jit(solution)/shard_map/ppermute | solution.py:12
  20.2 22.3 %collective-permute-start.1 = (bf16[256,512]{1,0:T(8,128)(2,1)}, bf16[256,512]{1,0:T(8,128)(2,1)}, u32[]{:S(2)}, u32[]{:S(2)}) collective-permute-start(bf16[256,512]{1,0:T(8,128)(2,1)} %get-tuple-element.29), channel_id=1, source_target_pairs={{0,7},{1,0},{2,1},{3,2},{4,3},{5,4},{6,5},{7,6},{8,15},{9,8},{10,9... | collective-permute-start | bytes 786440 | tf_op jit(solution)/shard_map/ppermute | solution.py:12
  24.8 16.8 %collective-permute-start = (bf16[256,512]{1,0:T(8,128)(2,1)}, bf16[256,512]{1,0:T(8,128)(2,1)}, u32[]{:S(2)}, u32[]{:S(2)}) collective-permute-start(bf16[256,512]{1,0:T(8,128)(2,1)} %get-tuple-element.30), channel_id=1, source_target_pairs={{0,1},{1,2},{2,3},{3,4},{4,5},{5,6},{6,7},{7,0},{8,9},{9,10},{10,1... | collective-permute-start | bytes 786440 | tf_op jit(solution)/shard_map/ppermute | solution.py:12
  24.9 4.2 copy-start.69
  33.6 3.0 copy-start.51
  43.6 5.1 copy-start.59
  43.6 5.1 copy-start.65
  53.6 4.2 copy-start.47
  60.1 14.8 %copy-start.53 = (s32[1024]{0:T(1024)S(1)}, s32[1024]{0:T(1024)}, u32[]{:S(2)}) copy-start(s32[1024]{0:T(1024)} %get-tuple-element.59) | copy-start | bytes 12292
  61.5 18.1 %collective-permute-start.4 = (bf16[64,512]{1,0:T(8,128)(2,1)S(1)}, bf16[64,512]{1,0:T(8,128)(2,1)S(1)}, u32[]{:S(2)}, u32[]{:S(2)}) collective-permute-start(bf16[64,512]{1,0:T(8,128)(2,1)S(1)} %get-tuple-element.39), channel_id=1, source_target_pairs={{0,1},{1,2},{2,3},{3,4},{4,5},{5,6},{6,7},{7,0},{8,9},{9,10},{10,1... | collective-permute-start | bytes 196616 | tf_op jit(solution)/shard_map/ppermute | solution.py:12
  62.4 17.4 %all-to-all-start = ((bf16[32,4,512]{2,1,0:T(4,128)(2,1)}), bf16[32,4,512]{2,1,0:T(4,128)(2,1)S(1)}, u32[]{:S(2)}, u32[]{:S(2)}) async-start(bf16[32,4,512]{2,1,0:T(4,128)(2,1)} %broadcast_select_fusion.3), calls=%async_computation | async-start | bytes 262144 | tf_op jit(solution)/shard_map/all_to_all | solution.py:84
  68.5 11.2 %collective-permute-start.7 = (bf16[64,512]{1,0:T(8,128)(2,1)S(1)}, bf16[64,512]{1,0:T(8,128)(2,1)S(1)}, u32[]{:S(2)}, u32[]{:S(2)}) collective-permute-start(bf16[64,512]{1,0:T(8,128)(2,1)S(1)} %get-tuple-element.36), channel_id=1, source_target_pairs={{0,24},{8,0},{16,8},{24,16},{1,25},{9,1},{17,9},{25,17},{2,26},{10... | collective-permute-start | bytes 196616 | tf_op jit(solution)/shard_map/ppermute | solution.py:12
  70.1 9.6 %collective-permute-start.6 = (bf16[64,512]{1,0:T(8,128)(2,1)S(1)}, bf16[64,512]{1,0:T(8,128)(2,1)S(1)}, u32[]{:S(2)}, u32[]{:S(2)}) collective-permute-start(bf16[64,512]{1,0:T(8,128)(2,1)S(1)} %get-tuple-element.37), channel_id=1, source_target_pairs={{0,8},{8,16},{16,24},{24,0},{1,9},{9,17},{17,25},{25,1},{2,10},{10... | collective-permute-start | bytes 196616 | tf_op jit(solution)/shard_map/ppermute | solution.py:12
  70.1 9.6 %collective-permute-start.5 = (bf16[64,512]{1,0:T(8,128)(2,1)S(1)}, bf16[64,512]{1,0:T(8,128)(2,1)S(1)}, u32[]{:S(2)}, u32[]{:S(2)}) collective-permute-start(bf16[64,512]{1,0:T(8,128)(2,1)S(1)} %get-tuple-element.38), channel_id=1, source_target_pairs={{0,7},{1,0},{2,1},{3,2},{4,3},{5,4},{6,5},{7,6},{8,15},{9,8},{10,9... | collective-permute-start | bytes 196616 | tf_op jit(solution)/shard_map/ppermute | solution.py:12
  74.8 5.0 copy-start.55
  79.8 4.0 copy-start.61
  79.8 4.0 copy-start.70
  83.8 4.2 copy-start.21
  88.0 3.1 copy-start.43
  91.9 3.9 copy-start.19
  91.9 3.1 copy-start.34
  93.3 3.9 copy-start.38
  104.4 2.9 copy-start.50
  104.4 2.9 copy-start.62
  107.3 2.8 copy-start.6
  110.1 2.9 copy-start.80
  110.9 6.2 copy-start.28
  117.1 20.3 %copy-start.10 = (bf16[1024,512]{1,0:T(8,128)(2,1)}, bf16[1024,512]{1,0:T(8,128)(2,1)S(1)}, u32[]{:S(2)}) copy-start(bf16[1024,512]{1,0:T(8,128)(2,1)S(1)} %get-tuple-element.52) | copy-start | bytes 3145732
  127.9 19.5 %all-to-all-start.1 = ((bf16[32,4,512]{2,1,0:T(4,128)(2,1)}), bf16[32,4,512]{2,1,0:T(4,128)(2,1)S(1)}, u32[]{:S(2)}, u32[]{:S(2)}) async-start(bf16[32,4,512]{2,1,0:T(4,128)(2,1)} %reshape.209), calls=%async_computation.1 | async-start | bytes 262144 | tf_op jit(solution)/shard_map/all_to_all | solution.py:88
  130.8 270.0 %all-reduce.6.cloned.1.call-start = ((), (), s32[]{:S(2)}) async-start(), calls=%async_computation.3 | async-start | bytes 14680064 | tf_op jit(solution)/shard_map/psum | solution.py:202
  130.9 8.3 %collective-permute-start.8 = (bf16[64,512]{1,0:T(8,128)(2,1)}, bf16[64,512]{1,0:T(8,128)(2,1)S(1)}, u32[]{:S(2)}, u32[]{:S(2)}) collective-permute-start(bf16[64,512]{1,0:T(8,128)(2,1)} %get-tuple-element.31), channel_id=1, source_target_pairs={{0,7},{1,0},{2,1},{3,2},{4,3},{5,4},{6,5},{7,6},{8,15},{9,8},{10,9... | collective-permute-start | bytes 196616 | tf_op jit(solution)/shard_map/ppermute | solution.py:12
  135.5 3.9 collective-permute-start.11
  135.5 4.0 collective-permute-start.10
  137.2 7.4 %collective-permute-start.9 = (bf16[64,512]{1,0:T(8,128)(2,1)}, bf16[64,512]{1,0:T(8,128)(2,1)}, u32[]{:S(2)}, u32[]{:S(2)}) collective-permute-start(bf16[64,512]{1,0:T(8,128)(2,1)} %get-tuple-element.34), channel_id=1, source_target_pairs={{0,1},{1,2},{2,3},{3,4},{4,5},{5,6},{6,7},{7,0},{8,9},{9,10},{10,1... | collective-permute-start | bytes 196616 | tf_op jit(solution)/shard_map/ppermute | solution.py:12
  147.3 4.4 copy-start.27
  147.3 4.4 copy-start.29
  150.4 3.0 copy-start.16
  151.7 3.1 copy-start.20
  153.4 2.8 copy-start.24
  153.4 2.8 copy-start.35
  153.4 2.8 copy-start.39
  157.7 4.2 copy-start.52
  157.8 386.0 %all-reduce.4.cloned.1.call-start = ((), (), s32[]{:S(2)}) async-start(), calls=%async_computation.2 | async-start | bytes 6291456 | tf_op jit(solution)/shard_map/psum | solution.py:220
  166.8 3.1 copy-start.3
  166.8 3.1 copy-start.48
  166.8 3.1 copy-start.60
  188.0 12.4 %collective-permute-start.12 = (bf16[256,512]{1,0:T(8,128)(2,1)S(1)}, bf16[256,512]{1,0:T(8,128)(2,1)S(1)}, u32[]{:S(2)}, u32[]{:S(2)}) collective-permute-start(bf16[256,512]{1,0:T(8,128)(2,1)S(1)} %get-tuple-element.23), channel_id=1, source_target_pairs={{0,7},{1,0},{2,1},{3,2},{4,3},{5,4},{6,5},{7,6},{8,15},{9,8},{10,9... | collective-permute-start | bytes 786440 | tf_op jit(solution)/shard_map/ppermute | solution.py:12
  188.5 11.9 %collective-permute-start.15 = (bf16[256,512]{1,0:T(8,128)(2,1)S(1)}, bf16[256,512]{1,0:T(8,128)(2,1)S(1)}, u32[]{:S(2)}, u32[]{:S(2)}) collective-permute-start(bf16[256,512]{1,0:T(8,128)(2,1)S(1)} %get-tuple-element.24), channel_id=1, source_target_pairs={{0,8},{8,16},{16,24},{24,0},{1,9},{9,17},{17,25},{25,1},{2,10},{10... | collective-permute-start | bytes 786440 | tf_op jit(solution)/shard_map/ppermute | solution.py:12
  188.5 11.9 %collective-permute-start.14 = (bf16[256,512]{1,0:T(8,128)(2,1)S(1)}, bf16[256,512]{1,0:T(8,128)(2,1)S(1)}, u32[]{:S(2)}, u32[]{:S(2)}) collective-permute-start(bf16[256,512]{1,0:T(8,128)(2,1)S(1)} %get-tuple-element.25), channel_id=1, source_target_pairs={{0,24},{8,0},{16,8},{24,16},{1,25},{9,1},{17,9},{25,17},{2,26},{10... | collective-permute-start | bytes 786440 | tf_op jit(solution)/shard_map/ppermute | solution.py:12
  190.2 17.3 %collective-permute-start.13 = (bf16[256,512]{1,0:T(8,128)(2,1)S(1)}, bf16[256,512]{1,0:T(8,128)(2,1)}, u32[]{:S(2)}, u32[]{:S(2)}) collective-permute-start(bf16[256,512]{1,0:T(8,128)(2,1)S(1)} %get-tuple-element.26), channel_id=1, source_target_pairs={{0,1},{1,2},{2,3},{3,4},{4,5},{5,6},{6,7},{7,0},{8,9},{9,10},{10,1... | collective-permute-start | bytes 786440 | tf_op jit(solution)/shard_map/ppermute | solution.py:12
  194.5 13.0 %slice-start = ((f32[1536,512]{1,0:T(8,128)}), f32[512,512]{1,0:T(8,128)S(1)}, s32[]{:S(2)}) async-start(f32[1536,512]{1,0:T(8,128)} %scatter_custom_fusion.3), calls=%async_computation.5 | async-start | bytes 2097152 | tf_op jit(solution)/shard_map/slice | solution.py:214
  194.5 21.1 %copy-start.33 = (bf16[512,512]{1,0:T(8,128)(2,1)S(1)}, bf16[512,512]{1,0:T(8,128)(2,1)}, u32[]{:S(2)}) copy-start(bf16[512,512]{1,0:T(8,128)(2,1)} %param.18) | copy-start | bytes 1572868
  218.9 462.7 %all-reduce.8.cloned.1.call-start = ((), (), s32[]{:S(2)}) async-start(), calls=%async_computation.4 | async-start | bytes 14680064 | tf_op jit(solution)/shard_map/psum | solution.py:202
  407.5 274.1 %copy-start.72 = (f32[10]{0:T(128)S(1)}, f32[10]{0:T(128)}, u32[]{:S(2)}) copy-start(f32[10]{0:T(128)} %constant.95.clone) | copy-start | bytes 124
  689.4 8.0 %copy-start.1 = (bf16[1024,512]{1,0:T(8,128)(2,1)S(1)}, bf16[1024,512]{1,0:T(8,128)(2,1)}, u32[]{:S(2)}) copy-start(bf16[1024,512]{1,0:T(8,128)(2,1)} %param.20) | copy-start | bytes 3145732
  (39 other events, 68.8 us)
Sparse Core Ops, SparseCore 0:
  157.9 242.9 all-reduce.5
  406.9 136.8 all-reduce.3
  546.2 135.3 all-reduce.7
